TPU v7x, 512 devices: a whole 4x4x16 slice. The times are simulated.
512 devices in a mesh: dp: 32 (over z, core), mp: 16 (over y, x).
Axes of the slice: x: 4, y: 4, z: 16, core: 2. Of those that a mesh axis runs over, the one named last changes fastest.
Arguments:
- token_ids: int32 [32768], P('dp'), may hold values from 0 to 128255
- lengths: int32 [256], P('dp'), may hold values from 1 to 128
- embed_grads: bfloat16 [32768, 4096], P('dp', 'mp'), may hold values from -6 to 6
- vocab_basis: bfloat16 [128256, 32], P('mp'), may hold values from -6 to 6
- embed_basis: bfloat16 [4096, 32], P('mp'), may hold values from -0.09375 to 0.09375
- layer_inputs: bfloat16 [1, 32768, 4096], P(None, 'dp', 'mp'), may hold values from -6 to 6
- layer_grads: bfloat16 [1, 32768, 4096], P(None, 'dp', 'mp'), may hold values from -6 to 6
- input_basis: bfloat16 [1, 4096, 32], P(None, 'mp'), may hold values from -0.09375 to 0.09375
- output_basis: bfloat16 [1, 4096, 32], P(None, 'mp'), may hold values from -0.09375 to 0.09375
- queries: bfloat16 [2, 1024, 256], P(None, 'mp', 'dp'), may hold values from -0.19921875 to 0.19921875
Outputs:
- scores: float32 [256, 256], P('dp')
All inputs are finite; a program needn't handle non-finite values.
Results may differ from a plain program's by a relative error of at most 0.0003.
Values may be sent and summed in bfloat16 or wider, within the bound.
A program may use at most 64 MiB of HBM per device.

v0:
```python
import jax
import jax.numpy as jnp
from jax import lax
from jax.sharding import PartitionSpec as P

ITERS = 2


damping = 0.01
epsilon = 1e-06
highest = lax.Precision.HIGHEST


def cut_along(shard, dim, peers):
    before, after = (shard.shape[:dim], shard.shape[dim + 1 :])
    return jnp.moveaxis(shard.reshape(*before, peers, -1, *after), dim, 0)


def sent_and_summed(shard, axis, dim):
    parts = cut_along(shard, dim, lax.axis_size(axis))
    arrived = lax.all_to_all(parts, axis, split_axis=0, concat_axis=0, tiled=True)
    return arrived.sum(axis=0)


def from_everyone(shard, axis):
    copies = jnp.broadcast_to(shard, (lax.axis_size(axis), *shard.shape))
    return lax.all_to_all(copies, axis, split_axis=0, concat_axis=0, tiled=True)


def taken_together(shard, axis):
    return from_everyone(shard, axis).sum(axis=0)


def joined_along(parts, dim):
    lengths = list(parts.shape[1:])
    lengths[dim] *= parts.shape[0]
    return jnp.moveaxis(parts, 0, dim).reshape(lengths)


def gathered_copies(shard, axis, dim):
    parts = from_everyone(shard, axis)
    return joined_along(parts, dim)


def solve_columns(right_side, apply_operator, column_norm, column_curve):
    solution = jnp.zeros_like(right_side)
    residual = right_side
    direction = right_side
    norm_now = column_norm(residual)
    for iteration in range(ITERS):
        images = apply_operator(direction)
        step_size = norm_now / (column_curve(direction, images) + epsilon)
        solution = solution + step_size[:, None, :] * direction
        residual = residual - step_size[:, None, :] * images
        norm_next = column_norm(residual)
        direction = residual + (norm_next / (norm_now + epsilon))[:, None, :] * direction
        norm_now = norm_next
    return solution


def per_device(
    token_ids,
    lengths,
    embed_grads,
    vocab_basis,
    embed_basis,
    layer_inputs,
    layer_grads,
    input_basis,
    output_basis,
    queries,
):
    vocab_rows = vocab_basis.shape[0]
    basis_rank = embed_basis.shape[1]
    layer_count = layer_inputs.shape[0] + 1
    seq_count = lengths.shape[0]
    token_count = token_ids.shape[0]
    slot_len = token_count // seq_count
    sketch_len = basis_rank * basis_rank
    mp_index = lax.axis_index("mp")
    local_ids = token_ids - mp_index * vocab_rows
    inside = (local_ids >= 0) & (local_ids < vocab_rows)
    looked = jnp.take(vocab_basis, jnp.clip(local_ids, 0, vocab_rows - 1), axis=0)
    pieces = [
        jnp.dot(embed_grads, embed_basis, preferred_element_type=jnp.float32),
        jnp.where(inside[:, None], looked.astype(jnp.float32), 0.0),
    ]
    pieces.append(jnp.dot(layer_grads[0], output_basis[0], preferred_element_type=jnp.float32))
    pieces.append(jnp.dot(layer_inputs[0], input_basis[0], preferred_element_type=jnp.float32))
    projected = jnp.concatenate(pieces, axis=1)
    inverse_len = 1.0 / lengths.astype(jnp.float32)
    share_rows = sent_and_summed(projected, "mp", 0)
    share_count = share_rows.shape[0]
    row_ids = mp_index * share_count + jnp.arange(share_count, dtype=jnp.int32)
    owner_seq = row_ids // slot_len
    position = row_ids % slot_len
    member = owner_seq[None, :] == jnp.arange(seq_count, dtype=jnp.int32)[:, None]
    is_live = position[None, :] < lengths[:, None]
    weights = jnp.where(member & is_live, inverse_len[:, None], 0.0)
    layout = share_rows.reshape(share_count, layer_count, 2, basis_rank)
    outer_rows = (layout[:, :, 0, :, None] * layout[:, :, 1, None, :]).reshape(
        share_count, layer_count, sketch_len
    )
    partial_sk = jnp.einsum("st,tlk->lsk", weights, outer_rows, precision=highest)
    sketches = taken_together(partial_sk, "mp")
    examples = seq_count * lax.axis_size("dp")
    targets = gathered_copies(queries, "dp", 2)
    everyone = lax.all_gather(sketches, "dp", axis=1, tiled=True)
    columns = lax.all_to_all(targets, "mp", split_axis=2, concat_axis=1, tiled=True)

    def apply_sketch(direction):
        inner_sums = jnp.einsum("lek,lkq->leq", everyone, direction, precision=highest)
        back_proj = jnp.einsum("lek,leq->lkq", everyone, inner_sums, precision=highest)
        return back_proj / examples + damping * direction

    def local_norm(residual):
        return jnp.sum(residual * residual, axis=1)

    def local_curve(direction, images):
        return jnp.sum(direction * images, axis=1)

    solution = solve_columns(columns.astype(jnp.float32), apply_sketch, local_norm, local_curve)
    partial_value = jnp.einsum("lek,lkq->eq", sketches, solution, precision=highest)
    scores = gathered_copies(partial_value, "mp", 1)
    return scores


def solution(mesh):
    placed = (
        P("dp"),
        P("dp"),
        P("dp", "mp"),
        P("mp", None),
        P("mp", None),
        P(None, "dp", "mp"),
        P(None, "dp", "mp"),
        P(None, "mp", None),
        P(None, "mp", None),
        P(None, "mp", "dp"),
    )
    return jax.shard_map(
        per_device, mesh=mesh, in_specs=placed, out_specs=P("dp", None), check_vma=False
    )
```

profile of v0, /device:TPU:1, one launch (start us, length us, event | category | flops | bytes accessed | tf_op | source)
XLA Modules:
  0.0 159.7 jit_solution(17661469512757702283)
XLA Ops:
  6.5 0.8 compare_and_fusion.1
  7.3 0.7 fusion.25
  8.0 2.3 %copy.38 = bf16[8016,32]{1,0:T(8,128)(2,1)S(1)} copy(bf16[8016,32]{0,1:T(8,128)(2,1)} %param.13) | data formatting | bytes 1026048 | tf_op args[3]
  10.4 3.2 %gather_fusion = bf16[1024,32]{1,0:T(8,128)(2,1)S(1)} fusion(bf16[8016,32]{1,0:T(8,128)(2,1)S(1)} %copy.38, s32[1024]{0:T(1024)S(1)} %fusion.25), kind=kCustom, calls=%fused_computation | custom fusion | bytes 135168 | tf_op jit(solution)/shard_map/jit(_take)/gather | solution.py:83
  14.0 0.2 fusion.4
  14.3 1.3 fusion.6
  15.6 1.0 copy.40
  16.6 7.6 %all-to-all-start = ((f32[16,64,128]{2,1,0:T(8,128)}), f32[16,64,128]{2,1,0:T(8,128)S(1)}, u32[]{:S(2)}, u32[]{:S(2)}) async-start(f32[16,64,128]{2,1,0:T(8,128)} %bitcast.4), calls=%async_computation | async-start | bytes 1048576 | tf_op jit(solution)/shard_map/all_to_all | solution.py:21
  24.3 8.9 %all-to-all-done = f32[16,64,128]{2,1,0:T(8,128)S(1)} async-done(((f32[16,64,128]{2,1,0:T(8,128)}), f32[16,64,128]{2,1,0:T(8,128)S(1)}, u32[]{:S(2)}, u32[]{:S(2)}) %all-to-all-start) | async-done | bytes 524320 | tf_op jit(solution)/shard_map/all_to_all | solution.py:21
  33.5 1.0 convolution_bitcast_fusion
  34.7 15.7 %all_to_all.38 = f32[16,2,8,1024]{3,2,1,0:T(8,128)S(1)} all-to-all(f32[16,2,8,1024]{3,2,1,0:T(8,128)S(1)} %broadcast_in_dim.62), channel_id=1, replica_groups=mesh['dp'=32,'mp'=16] {'mp'}, dimensions={0} | all-to-all | bytes 2097152 | tf_op jit(solution)/shard_map/all_to_all | solution.py:27
  50.4 0.7 reduce_sum.55
  51.3 35.3 %all_to_all.39 = bf16[32,2,512]{2,1,0:T(2,128)(2,1)S(1)} all-to-all(bf16[32,2,512]{2,1,0:T(2,128)(2,1)S(1)} %reshape.90), channel_id=1, replica_groups=mesh['dp'=32,'mp'=16] {'dp'}, dimensions={0} | all-to-all | bytes 131072 | tf_op jit(solution)/shard_map/all_to_all | solution.py:27
  87.1 9.1 %all_to_all.40 = bf16[16,2,1024]{2,1,0:T(2,128)(2,1)S(1)} all-to-all(bf16[16,2,1024]{2,1,0:T(2,128)(2,1)S(1)} %reshape.92), channel_id=1, replica_groups=mesh['dp'=32,'mp'=16] {'mp'}, dimensions={0} | all-to-all | bytes 131072 | tf_op jit(solution)/shard_map/all_to_all | solution.py:109
  96.7 33.9 %all-gather.2.cloned.1.call-done = f32[2,256,1024]{2,1,0:T(8,128)} async-done(((f32[2,8,1024]{2,1,0:T(8,128)}), f32[2,256,1024]{2,1,0:T(8,128)}) %all-gather.2.cloned.1.call-update) | async-done | bytes 2097168 | tf_op jit(solution)/shard_map/all_gather | solution.py:108
  130.6 2.8 %fusion.33 = f32[2,256,16]{1,2,0:T(8,128)S(1)} fusion(f32[2,256,1024]{2,1,0:T(8,128)} %all-gather.2.cloned.1.call-done, bf16[2,1024,16]{1,2,0:T(8,128)(2,1)S(1)} %all_to_all.31), kind=kOutput, calls=%fused_computation.64 | convolution fusion | flops 100663296 | bytes 2195456 | tf_op jit(solution)/shard_map/lek,lkq->leq/dot_general | solution.py:112
  133.4 1.3 fusion.8
  134.9 1.9 %fusion.16 = f32[2,256,16]{1,2,0:T(8,128)S(1)} fusion(f32[2,256,1024]{2,1,0:T(8,128)S(1)} %copy-done.1, bf16[2,1024,16]{1,2,0:T(8,128)(2,1)S(1)} %all_to_all.31, f32[2,1024,16]{1,2,0:T(8,128)S(1)} %get-tuple-element.10, f32[2,16]{1,0:T(2,128)S(1)} %add_divide_fusion.1, f32[2,16]{1,0:T(2,128)S(1)} %add_divide_fusion.2), kind=kOutput, calls=%fused_computation.30 | convolution fusion | flops 100827136 | bytes 2326784 | tf_op jit(solution)/shard_map/lek,lkq->leq/dot_general | solution.py:112
  136.8 1.3 fusion.3
  138.1 0.3 convolution_bitcast_fusion.1
  138.6 12.3 %all_to_all.41 = f32[16,1,128]{2,1,0:T(1,128)S(1)} all-to-all(f32[16,1,128]{2,1,0:T(1,128)S(1)} %reshape.94), channel_id=1, replica_groups=mesh['dp'=32,'mp'=16] {'mp'}, dimensions={0} | all-to-all | bytes 16384 | tf_op jit(solution)/shard_map/all_to_all | solution.py:27
  150.9 0.5 broadcast.125
  151.4 0.7 reduce.1
  152.2 0.7 reshape.78
  (50 shorter events, 2.4 us)
Async XLA Ops:
  6.5 7.2 %copy-start = (bf16[1024,256]{1,0:T(8,128)(2,1)S(1)}, bf16[1024,256]{1,0:T(8,128)(2,1)}, u32[]{:S(2)}) copy-start(bf16[1024,256]{1,0:T(8,128)(2,1)} %param.12) | copy-start | bytes 1572868
  8.0 5.7 %copy-start.4 = (bf16[256,32]{0,1:T(8,128)(2,1)S(1)}, bf16[256,32]{0,1:T(8,128)(2,1)}, u32[]{:S(2)}) copy-start(bf16[256,32]{0,1:T(8,128)(2,1)} %param.14) | copy-start | bytes 49156
  10.3 3.6 %copy-start.2 = (bf16[1,1024,256]{2,1,0:T(8,128)(2,1)S(1)}, bf16[1,1024,256]{2,1,0:T(8,128)(2,1)}, u32[]{:S(2)}) copy-start(bf16[1,1024,256]{2,1,0:T(8,128)(2,1)} %param.15) | copy-start | bytes 1572868
  10.3 3.6 %copy-start.5 = (bf16[1,256,32]{1,2,0:T(8,128)(2,1)S(1)}, bf16[1,256,32]{1,2,0:T(8,128)(2,1)}, u32[]{:S(2)}) copy-start(bf16[1,256,32]{1,2,0:T(8,128)(2,1)} %param.17) | copy-start | bytes 49156
  10.3 3.9 %copy-start.6 = (bf16[1,256,32]{1,2,0:T(8,128)(2,1)S(1)}, bf16[1,256,32]{1,2,0:T(8,128)(2,1)}, u32[]{:S(2)}) copy-start(bf16[1,256,32]{1,2,0:T(8,128)(2,1)} %param.18) | copy-start | bytes 49156
  14.2 10.1 %copy-start.8 = (s32[8]{0:T(128)S(1)}, s32[8]{0:T(128)}, u32[]{:S(2)}) copy-start(s32[8]{0:T(128)} %param.11) | copy-start | bytes 100
  16.6 16.6 %all-to-all-start = ((f32[16,64,128]{2,1,0:T(8,128)}), f32[16,64,128]{2,1,0:T(8,128)S(1)}, u32[]{:S(2)}, u32[]{:S(2)}) async-start(f32[16,64,128]{2,1,0:T(8,128)} %bitcast.4), calls=%async_computation | async-start | bytes 1048576 | tf_op jit(solution)/shard_map/all_to_all | solution.py:21
  24.2 106.4 %all-gather.2.cloned.1.call-start = ((), (), s32[]{:S(2)}) async-start(), calls=%async_computation.5 | async-start | bytes 2162688 | tf_op jit(solution)/shard_map/all_gather | solution.py:108
  34.6 16.6 %copy-start.7 = (bf16[2,64,8]{1,2,0:T(8,128)(2,1)S(1)}, bf16[2,64,8]{1,2,0:T(8,128)(2,1)}, u32[]{:S(2)}) copy-start(bf16[2,64,8]{1,2,0:T(8,128)(2,1)} %param.19) | copy-start | bytes 6148
  130.6 2.8 %copy-start.1 = (f32[2,256,1024]{2,1,0:T(8,128)S(1)}, f32[2,256,1024]{2,1,0:T(8,128)}, u32[]{:S(2)}) copy-start(f32[2,256,1024]{2,1,0:T(8,128)} %all-gather.2.cloned.1.call-done) | copy-start | bytes 6291460
  134.9 3.2 %copy-start.3 = (f32[2,8,1024]{2,1,0:T(8,128)S(1)}, f32[2,8,1024]{2,1,0:T(8,128)}, u32[]{:S(2)}) copy-start(f32[2,8,1024]{2,1,0:T(8,128)} %reduce_sum.55) | copy-start | bytes 196612
Sparse Core Ops, SparseCore 0:
  51.2 79.2 all-gather.1
where the time goes:
time: 160 us
  blocking collectives  72.5 us (45%)
  waiting for transfers between devices  42.9 us (27%)
  between operations  13.7 us (9%)
  matrix products  10.4 us (6%)
  local copies, waits for them, and re-layouts  9.29 us (6%)
  starting transfers between devices  7.62 us (5%)
  other arithmetic  3.36 us (2%)
    all_to_all x3, blocking collectives, from_everyone(): return lax.all_to_all(copies, axis, split_axis=0, concat_axis=0, tiled=True)  63.4 us
    all_gather x1, waiting for transfers between devices, per_device(): everyone = lax.all_gather(sketches, 'dp', axis=1, tiled=True)  33.9 us
    all_to_all x1, blocking collectives, per_device(): lax.all_to_all(targets, 'mp', split_axis=2, concat_axis=1, tiled=True)  9.14 us
    all_to_all x1, waiting for transfers between devices, sent_and_summed(): lax.all_to_all(parts, axis, split_axis=0, concat_axis=0, tiled=True)  8.95 us
    all_to_all x1, starting transfers between devices, sent_and_summed(): lax.all_to_all(parts, axis, split_axis=0, concat_axis=0, tiled=True)  7.57 us
    dot_general x2, matrix products, apply_sketch(): jnp.einsum('lek,lkq->leq', everyone, direction, precision=highest)  4.69 us
    gather x2, local copies, waits for them, and re-layouts, per_device(): jnp.take(vocab_basis, jnp.clip(local_ids, 0, vocab_rows - 1), axis=0)  3.32 us
  transfers between devices with their start and end apart: 2, of which 2 were waited for; matrix products, arithmetic and copies ran while one was open for 1% of the time, Pallas kernels for 0%

commit v1 on v0

v1 whole, which is shorter than its diff:
```python
import functools

import jax
import jax.numpy as jnp
from jax import lax
from jax.experimental import pallas as pl
from jax.experimental.pallas import tpu as pltpu
from jax.sharding import PartitionSpec as P

DAMPING = 0.01
EPSILON = 1e-06
MESH = pl.DeviceIdType.MESH
F32 = jnp.float32
BF16 = jnp.bfloat16

ZS = 16
MS = 16
REACH = 4
OWN = 7
BLK = 512


def dot_t(a, b):
    return lax.dot_general(a, b, (((1,), (1,)), ((), ())), preferred_element_type=F32)


def dot_n(a, b):
    return lax.dot_general(a, b, (((1,), (0,)), ((), ())), preferred_element_type=F32)


def halves(a):
    high = a.astype(BF16)
    return high, (a - high.astype(F32)).astype(BF16)


def kernel(
    ids_hbm, len_hbm, g0_hbm, vt_hbm, we_hbm, x1_hbm, g1_hbm, wi_hbm, wo_hbm, q_hbm,
    out_ref,
    ids, lens, g0, vt, we, x1, g1, wi, wo, q,
    last, table, send, recv, sk, qz, qg, sg, bt, bb, sh, sl, part, other,
    in_sem, a_send, a_recv, qz_send, qz_recv, qp_send, qp_recv, qs_send, qs_recv,
    sz_send, sz_recv, sp_send, sp_recv, ss_send, ss_recv, c_send, c_recv,
):
    d = lax.axis_index("dp")
    m = lax.axis_index("mp")
    core = d % 2
    z = d // 2
    x = m % 4
    layer = x // 2
    row = (m // 4) * 2 + x % 2
    sibling = (d + 1 - 2 * core, m)
    partner = (d, m - x + 3 - x)

    def along_z(offset):
        return (2 * ((z + offset + ZS) % ZS) + core, m)

    def in_plane(r):
        return (d, (m + r) % MS)

    def group_row(r):
        return (row + r) % 8

    def in_group(r):
        there = group_row(r)
        return (d, (there // 2) * 4 + 2 * layer + there % 2)

    pairs = [
        (ids_hbm, ids), (vt_hbm, vt), (q_hbm, q), (we_hbm, we), (g0_hbm, g0), (wo_hbm, wo),
        (g1_hbm, g1), (wi_hbm, wi), (x1_hbm, x1), (len_hbm, lens),
    ]
    loads = {}
    for n, (src, dst) in enumerate(pairs):
        loads[n] = pltpu.make_async_copy(src, dst, in_sem.at[n])
        loads[n].start()

    barrier = pltpu.get_barrier_semaphore()
    z_offsets = [o for k in range(1, REACH + 1) for o in (k, -k)]
    peers = [in_plane(r) for r in range(1, MS)] + [along_z(o) for o in z_offsets] + [sibling]
    for peer in peers:
        pl.semaphore_signal(barrier, inc=1, device_id=peer, device_id_type=MESH)

    def remote(src, dst, send_sem, recv_sem, peer):
        return pltpu.make_async_remote_copy(
            src_ref=src, dst_ref=dst, send_sem=send_sem, recv_sem=recv_sem,
            device_id=peer, device_id_type=MESH,
        )

    sent = []

    def go(copy):
        copy.start()
        sent.append(copy)

    loads[0].wait()
    loads[1].wait()
    full = vt.shape[1] // BLK
    rest = vt.shape[1] - full * BLK
    last[...] = jnp.zeros(last.shape, BF16)
    last[:, :rest] = vt[:, full * BLK:]
    for b in range(full):
        table[b * 32:(b + 1) * 32, :] = vt[:, b * BLK:(b + 1) * BLK]
    table[full * 32:(full + 1) * 32, :] = last[...]
    local = ids[...] - m * vt.shape[1]
    for p in range(4):
        mine = local[:, 256 * p:256 * (p + 1)]
        low = mine & (BLK - 1)
        high = mine >> 9
        spot = lax.broadcasted_iota(jnp.int32, (BLK, 256), 0)
        hot = jnp.where(spot == low, 1.0, 0.0).astype(BF16)
        looked = dot_n(table[...], hot)
        total = jnp.zeros((32, 256), F32)
        for b in range(full + 1):
            total = total + jnp.where(high == b, looked[b * 32:(b + 1) * 32, :], 0.0)
        for h in range(2):
            seq = 2 * p + h
            send[(seq // 2) * 4 + seq % 2, 32:64, :] = total[:, 128 * h:128 * (h + 1)]

    def project(basis, tokens, layer_at, first):
        out = dot_t(basis[...], tokens[...])
        for seq in range(8):
            send[(seq // 2) * 4 + 2 * layer_at + seq % 2, first:first + 32, :] = (
                out[:, 128 * seq:128 * (seq + 1)]
            )

    loads[3].wait()
    loads[4].wait()
    project(we, g0, 0, 0)
    loads[5].wait()
    loads[6].wait()
    project(wo, g1, 1, 0)
    loads[7].wait()
    loads[8].wait()
    project(wi, x1, 1, 32)
    loads[2].wait()
    loads[9].wait()
    qz[OWN] = jnp.concatenate([q[0].astype(F32), q[1].astype(F32)], axis=1).astype(BF16)

    pl.semaphore_wait(barrier, len(peers))

    for n, o in enumerate(z_offsets):
        go(remote(qz.at[OWN], qz.at[OWN - o], qz_send.at[n], qz_recv.at[n], along_z(o)))
    a_in = []
    for r in range(1, MS):
        there = (m + r) % MS
        copy = remote(send.at[there], recv.at[r - 1], a_send.at[r - 1], a_recv.at[r - 1], in_plane(r))
        go(copy)
        a_in.append(copy)

    def arrived_z(buffer, sems, n, o):
        remote(buffer.at[OWN], buffer.at[OWN - o], sems.at[n], sems.at[n], along_z(o)).wait_recv()

    for n, o in enumerate(z_offsets):
        arrived_z(qz, qz_recv, n, o)
    q_up = remote(qz.at[8:12], qz.at[12:16], qz_send.at[8], qz_recv.at[8], along_z(-REACH))
    q_down = remote(qz.at[4:7], qz.at[0:3], qz_send.at[9], qz_recv.at[9], along_z(REACH))
    go(q_up)
    go(q_down)

    for copy in a_in:
        copy.wait_recv()
    summed = send[m]
    for r in range(MS - 1):
        summed = summed + recv[r]
    lane8 = lax.broadcasted_iota(jnp.int32, (1, 8), 1)
    length = jnp.sum(jnp.where(lane8 == row, lens[...], 0), axis=1, keepdims=True)
    place = lax.broadcasted_iota(jnp.int32, (1, 128), 1)
    weight = jnp.where(place < length, 1.0 / length.astype(F32), 0.0)
    sk[...] = lax.dot_general(
        summed[:32] * weight, summed[32:], (((1,), (1,)), ((), ())),
        precision=lax.Precision.HIGHEST, preferred_element_type=F32,
    )
    sg[row, core, OWN] = jnp.concatenate(
        [sk[pl.ds(a, 8, stride=4), :] for a in range(4)], axis=1
    )

    def mine_of(lo, hi):
        return sg.at[row, core, lo:hi]

    own = sg.at[row, core]
    for n, o in enumerate(z_offsets):
        go(remote(own.at[OWN], own.at[OWN - o], sz_send.at[n], sz_recv.at[n], along_z(o)))

    q_up.wait_recv()
    q_down.wait_recv()
    for r in range(1, MS):
        go(remote(qz, qg.at[m, :, core], qp_send.at[r - 1], qp_recv.at[r - 1], in_plane(r)))
    go(remote(qz, qg.at[m, :, core], qs_send.at[0], qs_recv.at[0], sibling))
    for s in range(ZS):
        qg[m, s, core] = qz[s]

    for n, o in enumerate(z_offsets):
        arrived_z(own, sz_recv, n, o)
    s_up = remote(mine_of(8, 12), mine_of(12, 16), sz_send.at[8], sz_recv.at[8], along_z(-REACH))
    s_down = remote(mine_of(4, 7), mine_of(0, 3), sz_send.at[9], sz_recv.at[9], along_z(REACH))
    go(s_up)
    go(s_down)
    chunks = ((3, 12), (12, 16), (0, 3))

    def spread(k):
        lo, hi = chunks[k]
        for r in range(1, 8):
            go(remote(mine_of(lo, hi), mine_of(lo, hi), sp_send.at[k, r - 1], sp_recv.at[k, r - 1], in_group(r)))
        go(remote(mine_of(lo, hi), mine_of(lo, hi), ss_send.at[k, 0], ss_recv.at[k, 0], sibling))

    spread(0)

    for r in range(1, MS):
        origin = (m - r + MS) % MS
        block = qg.at[origin, :, core]
        remote(qz, block, qp_send.at[r - 1], qp_recv.at[r - 1], in_plane(r)).wait_recv()
        go(remote(block, block, qs_send.at[r], qs_recv.at[r], sibling))

    s_up.wait_recv()
    spread(1)
    s_down.wait_recv()
    spread(2)

    for r in range(MS):
        origin = (m - r + MS) % MS
        block = qg.at[origin, :, 1 - core]
        remote(block, block, qs_send.at[r], qs_recv.at[r], sibling).wait_recv()
    lane = lax.broadcasted_iota(jnp.int32, (16, 128), 1)
    left = lane < 64

    @pl.loop(0, ZS)
    def _(there):
        slot = (there - z + OWN + ZS) % ZS
        for s in range(8):
            a = qg[2 * s, slot].reshape(16, 128).astype(F32)
            b = qg[2 * s + 1, slot].reshape(16, 128).astype(F32)
            even = jnp.where(left, a, pltpu.roll(b, 64, 1))
            odd = jnp.where(left, pltpu.roll(a, 64, 1), b)
            both = jnp.where(layer == 0, even, odd)
            start = pl.multiple_of(there * 16, 16)
            bt[pl.ds(start, 16), 128 * s:128 * (s + 1)] = both.astype(BF16)

    square = bt[...].astype(F32)
    square_high, square_low = halves(square * square)
    ones = jnp.ones((8, 1024), BF16)
    bb[...] = dot_t(ones, square_high) + dot_t(ones, square_low)

    for k, (lo, hi) in enumerate(chunks):
        for r in range(1, 8):
            block = sg.at[(row - r + 8) % 8, core, lo:hi]
            remote(block, block, sp_send.at[k, r - 1], sp_recv.at[k, r - 1], in_group(r)).wait_recv()
            go(remote(block, block, ss_send.at[k, r], ss_recv.at[k, r], sibling))
    for k, (lo, hi) in enumerate(chunks):
        for r in range(8):
            block = sg.at[(row - r + 8) % 8, 1 - core, lo:hi]
            remote(block, block, ss_send.at[k, r], ss_recv.at[k, r], sibling).wait_recv()

    for i in range(8):
        for c in range(2):
            for s in range(8):
                piece = sg[i, c, :, s, :]
                ph, plow = halves(piece)
                at = (2 * i + c) * 16
                sh[at:at + 16, 128 * s:128 * (s + 1)] = ph
                sl[at:at + 16, 128 * s:128 * (s + 1)] = plow

    s_high, s_low = sh[...], sl[...]
    u = dot_t(s_high, bt[...]) + dot_t(s_low, bt[...])
    k_mat = dot_t(s_high, s_high) + dot_t(s_high, s_low) + dot_t(s_low, s_high)
    k_high, k_low = halves(k_mat)
    u_high, u_low = halves(u)
    v = dot_n(k_high, u_high) + dot_n(k_high, u_low) + dot_n(k_low, u_high)

    rr = bb[0:1, :]
    scaled = u * 0.0625
    uu = jnp.sum(scaled * scaled, axis=0, keepdims=True)
    step0 = rr / (uu + DAMPING * rr + EPSILON)
    keep = 1.0 - DAMPING * step0
    au = (step0 * 0.00390625) * u
    av = (step0 * 0.00390625) * v
    auu = step0 * uu
    aauv = jnp.sum(au * av, axis=0, keepdims=True)
    new = jnp.maximum(keep * keep * rr - 2.0 * keep * auu + aauv, 0.0)
    fac = keep + new / (rr + EPSILON)
    dd = jnp.maximum(fac * fac * rr - 2.0 * fac * auu + aauv, 0.0)
    y = fac * u - av
    scaled_y = y * 0.0625
    yy = jnp.sum(scaled_y * scaled_y, axis=0, keepdims=True)
    step1 = new / (yy + DAMPING * dd + EPSILON)
    scores = step0 * u + step1 * y
    parts0 = [scores[(2 * i) * 16 + OWN:(2 * i) * 16 + OWN + 1, :] for i in range(8)]
    parts1 = [scores[(2 * i + 1) * 16 + OWN:(2 * i + 1) * 16 + OWN + 1, :] for i in range(8)]
    part[...] = jnp.where(core == 0, jnp.concatenate(parts0, axis=0), jnp.concatenate(parts1, axis=0))

    final = remote(part, other, c_send.at[0], c_recv.at[0], partner)
    go(final)
    final.wait_recv()
    out_ref[...] = part[...] + other[...]
    for copy in sent:
        copy.wait_send()


def per_device(
    token_ids, lengths, embed_grads, vocab_basis, embed_basis,
    layer_inputs, layer_grads, input_basis, output_basis, queries,
):
    vocab = vocab_basis.shape[0]
    dma = pltpu.SemaphoreType.DMA
    return pl.pallas_call(
        kernel,
        out_shape=jax.ShapeDtypeStruct((8, 256), F32),
        in_specs=[pl.BlockSpec(memory_space=pl.ANY)] * 10,
        out_specs=pl.BlockSpec(memory_space=pltpu.VMEM),
        scratch_shapes=[
            pltpu.VMEM((1, 1024), jnp.int32),
            pltpu.VMEM((1, 8), jnp.int32),
            pltpu.VMEM((1024, 256), BF16),
            pltpu.VMEM((32, vocab), BF16),
            pltpu.VMEM((32, 256), BF16),
            pltpu.VMEM((1024, 256), BF16),
            pltpu.VMEM((1024, 256), BF16),
            pltpu.VMEM((32, 256), BF16),
            pltpu.VMEM((32, 256), BF16),
            pltpu.VMEM((2, 8, 64), BF16),
            pltpu.VMEM((32, BLK), BF16),
            pltpu.VMEM((512, BLK), BF16),
            pltpu.VMEM((MS, 64, 128), F32),
            pltpu.VMEM((MS - 1, 64, 128), F32),
            pltpu.VMEM((32, 32), F32),
            pltpu.VMEM((ZS, 8, 128), BF16),
            pltpu.VMEM((MS, ZS, 2, 8, 128), BF16),
            pltpu.VMEM((8, 2, ZS, 8, 128), F32),
            pltpu.VMEM((256, 1024), BF16),
            pltpu.VMEM((8, 256), F32),
            pltpu.VMEM((256, 1024), BF16),
            pltpu.VMEM((256, 1024), BF16),
            pltpu.VMEM((8, 256), F32),
            pltpu.VMEM((8, 256), F32),
            dma((10,)),
            dma((MS - 1,)), dma((MS - 1,)),
            dma((10,)), dma((10,)),
            dma((MS - 1,)), dma((MS - 1,)),
            dma((MS,)), dma((MS,)),
            dma((10,)), dma((10,)),
            dma((3, 7)), dma((3, 7)),
            dma((3, 8)), dma((3, 8)),
            dma((1,)), dma((1,)),
        ],
        compiler_params=pltpu.CompilerParams(
            collective_id=0, has_side_effects=True, vmem_limit_bytes=48 * 1024 * 1024
        ),
        name="attribution",
    )(
        token_ids.reshape(1, -1), lengths.reshape(1, -1), embed_grads, vocab_basis.T, embed_basis.T,
        layer_inputs[0], layer_grads[0], input_basis[0].T, output_basis[0].T,
        queries.transpose(0, 2, 1),
    )


def solution(mesh):
    placed = (
        P("dp"),
        P("dp"),
        P("dp", "mp"),
        P("mp", None),
        P("mp", None),
        P(None, "dp", "mp"),
        P(None, "dp", "mp"),
        P(None, "mp", None),
        P(None, "mp", None),
        P(None, "mp", "dp"),
    )
    return jax.shard_map(
        per_device, mesh=mesh, in_specs=placed, out_specs=P("dp", None), check_vma=False
    )
```

time: 160 us -> 58 us (0.36)
  blocking collectives: 72.5 us -> 0 us
  Pallas kernels: 0 us -> 49.2 us
  waiting for transfers between devices: 42.9 us -> 0 us
  between operations: 13.7 us -> 0.02 us
  matrix products: 10.4 us -> 0 us
  starting transfers between devices: 7.62 us -> 0 us
  other arithmetic: 3.36 us -> 0 us
    all_to_all x4 -> x0, blocking collectives: 72.5 us -> none  [the longest x3 63.4 us: from_everyone(): return lax.all_to_all(copies, axis, split_axis=0, concat_axis=0, tiled=True)]
    pallas_call x0 -> x1, Pallas kernels: none -> 49.2 us  [per_device(): pl.pallas_call(kernel, out_shape=jax.ShapeDtypeStruct((8, 256), F32), in_...]
    all_gather x1 -> x0, waiting for transfers between devices: 33.9 us -> none  [per_device(): everyone = lax.all_gather(sketches, 'dp', axis=1, tiled=True)]
    dot_general x9 -> x0, matrix products: 10.4 us -> none  [the longest x2 4.69 us: apply_sketch(): jnp.einsum('lek,lkq->leq', everyone, direction, precision=highest)]
    all_to_all x1 -> x0, waiting for transfers between devices: 8.95 us -> none  [sent_and_summed(): lax.all_to_all(parts, axis, split_axis=0, concat_axis=0, tiled=True)]
    all_to_all x1 -> x0, starting transfers between devices: 7.57 us -> none  [sent_and_summed(): lax.all_to_all(parts, axis, split_axis=0, concat_axis=0, tiled=True)]
    unnamed x26 -> x21, local copies, waits for them, and re-layouts: 3.12 us -> 8.29 us
    gather x2 -> x0, local copies, waits for them, and re-layouts: 3.32 us -> none  [per_device(): jnp.take(vocab_basis, jnp.clip(local_ids, 0, vocab_rows - 1), axis=0)]
  transfers between devices with their start and end apart: 2 -> 0, of which waited for: 2 -> 0; matrix products, arithmetic and copies ran while one was open for 1% -> 0% of each run, Pallas kernels for 0% -> 0%
where the time goes in v1:
time: 58 us; the launch traced here: 57.5 us
  Pallas kernels  49.2 us (85%)
  local copies, waits for them, and re-layouts  8.29 us (14%)
    pallas_call x1, Pallas kernels, per_device(): pl.pallas_call(kernel, out_shape=jax.ShapeDtypeStruct((8, 256), F32), in_...  49.2 us
    unnamed x21, local copies, waits for them, and re-layouts  8.29 us

profile of v1, /device:TPU:1, one launch (start us, length us, event | category | flops | bytes accessed | tf_op | source)
XLA Modules:
  0.0 57.5 jit_solution(10463651198390355139)
XLA Ops:
  0.0 0.0 copy-start.4
  0.0 0.0 copy-start.9
  0.0 0.7 %copy-done.4 = bf16[256,32]{0,1:T(8,128)(2,1)S(1)} copy-done((bf16[256,32]{0,1:T(8,128)(2,1)S(1)}, bf16[256,32]{0,1:T(8,128)(2,1)}, u32[]{:S(2)}) %copy-start.4) | copy-done | bytes 16408
  0.7 0.0 copy-done.9
  0.7 0.0 copy-start
  0.7 1.0 %copy-done = bf16[1024,256]{1,0:T(8,128)(2,1)S(1)} copy-done((bf16[1024,256]{1,0:T(8,128)(2,1)S(1)}, bf16[1024,256]{1,0:T(8,128)(2,1)}, u32[]{:S(2)}) %copy-start) | copy-done | bytes 524312
  1.8 0.0 copy-start.1
  1.8 1.0 %copy-done.1 = bf16[1,1024,256]{2,1,0:T(8,128)(2,1)S(1)} copy-done((bf16[1,1024,256]{2,1,0:T(8,128)(2,1)S(1)}, bf16[1,1024,256]{2,1,0:T(8,128)(2,1)}, u32[]{:S(2)}) %copy-start.1) | copy-done | bytes 524312
  2.8 0.0 copy-start.2
  2.8 1.0 %copy-done.2 = bf16[1,1024,256]{2,1,0:T(8,128)(2,1)S(1)} copy-done((bf16[1,1024,256]{2,1,0:T(8,128)(2,1)S(1)}, bf16[1,1024,256]{2,1,0:T(8,128)(2,1)}, u32[]{:S(2)}) %copy-start.2) | copy-done | bytes 524312
  3.8 0.0 copy-start.3
  3.9 1.0 %copy-done.3 = bf16[8016,32]{0,1:T(8,128)(2,1)S(1)} copy-done((bf16[8016,32]{0,1:T(8,128)(2,1)S(1)}, bf16[8016,32]{0,1:T(8,128)(2,1)}, u32[]{:S(2)}) %copy-start.3) | copy-done | bytes 513048
  4.9 0.0 copy-start.5
  4.9 0.7 %copy-done.5 = bf16[1,256,32]{1,2,0:T(8,128)(2,1)S(1)} copy-done((bf16[1,256,32]{1,2,0:T(8,128)(2,1)S(1)}, bf16[1,256,32]{1,2,0:T(8,128)(2,1)}, u32[]{:S(2)}) %copy-start.5) | copy-done | bytes 16408
  5.6 0.0 copy-start.6
  5.6 0.7 %copy-done.6 = bf16[1,256,32]{1,2,0:T(8,128)(2,1)S(1)} copy-done((bf16[1,256,32]{1,2,0:T(8,128)(2,1)S(1)}, bf16[1,256,32]{1,2,0:T(8,128)(2,1)}, u32[]{:S(2)}) %copy-start.6) | copy-done | bytes 16408
  6.3 0.0 copy-start.7
  6.3 0.7 %copy-done.7 = s32[1024]{0:T(1024)S(1)} copy-done((s32[1024]{0:T(1024)S(1)}, s32[1024]{0:T(1024)}, u32[]{:S(2)}) %copy-start.7) | copy-done | bytes 4120
  7.0 0.0 copy-start.8
  7.0 0.7 %copy-done.8 = bf16[2,64,8]{1,2,0:T(8,128)(2,1)S(1)} copy-done((bf16[2,64,8]{1,2,0:T(8,128)(2,1)S(1)}, bf16[2,64,8]{1,2,0:T(8,128)(2,1)}, u32[]{:S(2)}) %copy-start.8) | copy-done | bytes 2072
  7.7 49.2 %attribution.1 = f32[8,256]{1,0:T(8,128)S(1)} custom-call(s32[1,1024]{1,0:T(1,128)S(1)} %bitcast.19, s32[1,8]{1,0:T(1,128)S(1)} %bitcast.21, bf16[1024,256]{1,0:T(8,128)(2,1)S(1)} %copy-done, bf16[32,8016]{1,0:T(8,128)(2,1)S(1)} %bitcast.15, bf16[32,256]{1,0:T(8,128)(2,1)S(1)} %bitcast.16, bf16[1024,256]{1,0:T(8,128)(2,1)S(1)} %bitcast.13, ...), custom_call_target="tpu_custom_call" | custom-call | tf_op jit(solution)/shard_map/attribution/pallas_call | solution.py:303
  56.9 0.6 %copy.12 = f32[8,256]{1,0:T(8,128)} copy(f32[8,256]{1,0:T(8,128)S(1)} %attribution.1) | data formatting | bytes 16384
Async XLA Ops:
  0.0 0.7 %copy-start.4 = (bf16[256,32]{0,1:T(8,128)(2,1)S(1)}, bf16[256,32]{0,1:T(8,128)(2,1)}, u32[]{:S(2)}) copy-start(bf16[256,32]{0,1:T(8,128)(2,1)} %param.14) | copy-start | bytes 49156
  0.0 0.7 %copy-start.9 = (s32[8]{0:T(128)S(1)}, s32[8]{0:T(128)}, u32[]{:S(2)}) copy-start(s32[8]{0:T(128)} %param.11) | copy-start | bytes 100
  0.7 1.0 %copy-start = (bf16[1024,256]{1,0:T(8,128)(2,1)S(1)}, bf16[1024,256]{1,0:T(8,128)(2,1)}, u32[]{:S(2)}) copy-start(bf16[1024,256]{1,0:T(8,128)(2,1)} %g0_hbm.1) | copy-start | bytes 1572868
  1.8 1.0 %copy-start.1 = (bf16[1,1024,256]{2,1,0:T(8,128)(2,1)S(1)}, bf16[1,1024,256]{2,1,0:T(8,128)(2,1)}, u32[]{:S(2)}) copy-start(bf16[1,1024,256]{2,1,0:T(8,128)(2,1)} %param.15) | copy-start | bytes 1572868
  2.8 1.0 %copy-start.2 = (bf16[1,1024,256]{2,1,0:T(8,128)(2,1)S(1)}, bf16[1,1024,256]{2,1,0:T(8,128)(2,1)}, u32[]{:S(2)}) copy-start(bf16[1,1024,256]{2,1,0:T(8,128)(2,1)} %param.16) | copy-start | bytes 1572868
  3.8 1.0 %copy-start.3 = (bf16[8016,32]{0,1:T(8,128)(2,1)S(1)}, bf16[8016,32]{0,1:T(8,128)(2,1)}, u32[]{:S(2)}) copy-start(bf16[8016,32]{0,1:T(8,128)(2,1)} %param.13) | copy-start | bytes 1539076
  4.9 0.7 %copy-start.5 = (bf16[1,256,32]{1,2,0:T(8,128)(2,1)S(1)}, bf16[1,256,32]{1,2,0:T(8,128)(2,1)}, u32[]{:S(2)}) copy-start(bf16[1,256,32]{1,2,0:T(8,128)(2,1)} %param.17) | copy-start | bytes 49156
  5.6 0.7 %copy-start.6 = (bf16[1,256,32]{1,2,0:T(8,128)(2,1)S(1)}, bf16[1,256,32]{1,2,0:T(8,128)(2,1)}, u32[]{:S(2)}) copy-start(bf16[1,256,32]{1,2,0:T(8,128)(2,1)} %param.18) | copy-start | bytes 49156
  6.3 0.7 %copy-start.7 = (s32[1024]{0:T(1024)S(1)}, s32[1024]{0:T(1024)}, u32[]{:S(2)}) copy-start(s32[1024]{0:T(1024)} %param.10) | copy-start | bytes 12292
  7.0 0.7 %copy-start.8 = (bf16[2,64,8]{1,2,0:T(8,128)(2,1)S(1)}, bf16[2,64,8]{1,2,0:T(8,128)(2,1)}, u32[]{:S(2)}) copy-start(bf16[2,64,8]{1,2,0:T(8,128)(2,1)} %param.19) | copy-start | bytes 6148

commit v2 on v1

v2 whole, which is shorter than its diff:
```python
import jax
import jax.numpy as jnp
from jax import lax
from jax.experimental import pallas as pl
from jax.experimental.pallas import tpu as pltpu
from jax.sharding import PartitionSpec as P

DAMPING = 0.01
EPSILON = 1e-06
MESH = pl.DeviceIdType.MESH
F32 = jnp.float32
BF16 = jnp.bfloat16

ZS = 16
MS = 16
REACH = 4
BLK = 512


def dot_t(a, b):
    return lax.dot_general(a, b, (((1,), (1,)), ((), ())), preferred_element_type=F32)


def dot_n(a, b):
    return lax.dot_general(a, b, (((1,), (0,)), ((), ())), preferred_element_type=F32)


def halves(a):
    high = a.astype(BF16)
    return high, (a - high.astype(F32)).astype(BF16)


def kernel(
    ids_hbm, len_hbm, g0_hbm, vt_hbm, we_hbm, x1_hbm, g1_hbm, wi_hbm, wo_hbm, q_hbm,
    out_ref,
    ids, lens, g0, vt, we, x1, g1, wi, wo, q,
    last, table, gsend, xsend, tsend, grecv, xrecv, trecv, xsum, sk,
    qz, qp, qg, sz, shl, bt, bb, part, other,
    in_sem, g_send, g_recv, x_send, x_recv, qz_send, qz_recv, qp_send, qp_recv, qs_send, qs_recv,
    sz_send, sz_recv, sp_send, sp_recv, ss_send, ss_recv, c_send, c_recv,
):
    d = lax.axis_index("dp")
    m = lax.axis_index("mp")
    core = d % 2
    z = d // 2
    x = m % 4
    layer = x // 2
    row = (m // 4) * 2 + x % 2
    sibling = (d + 1 - 2 * core, m)
    partner = (d, m - x + 3 - x)

    def along_z(offset):
        return (2 * ((z + offset + ZS) % ZS) + core, m)

    def in_plane(r):
        return (d, (m + r) % MS)

    def in_group(r):
        there = (row + r) % 8
        return (d, (there // 2) * 4 + 2 * layer + there % 2)

    pairs = [
        (q_hbm, q), (wo_hbm, wo), (g1_hbm, g1), (wi_hbm, wi), (x1_hbm, x1),
        (we_hbm, we), (g0_hbm, g0), (ids_hbm, ids), (vt_hbm, vt), (len_hbm, lens),
    ]
    loads = []
    for n, (src, dst) in enumerate(pairs):
        loads.append(pltpu.make_async_copy(src, dst, in_sem.at[n]))
        loads[n].start()

    barrier = pltpu.get_barrier_semaphore()
    z_offsets = [o for k in range(REACH, 0, -1) for o in (k, -k)]
    peers = [along_z(o) for o in z_offsets] + [in_plane(r) for r in range(1, MS)] + [sibling]
    for peer in peers:
        pl.semaphore_signal(barrier, inc=1, device_id=peer, device_id_type=MESH)

    def remote(src, dst, send_sem, recv_sem, peer):
        return pltpu.make_async_remote_copy(
            src_ref=src, dst_ref=dst, send_sem=send_sem, recv_sem=recv_sem,
            device_id=peer, device_id_type=MESH,
        )

    sent = []

    def go(copy):
        copy.start()
        sent.append(copy)

    def project(basis, tokens, layer_at, target):
        out = dot_t(basis[...], tokens[...])
        for seq in range(8):
            target[(seq // 2) * 4 + 2 * layer_at + seq % 2] = out[:, 128 * seq:128 * (seq + 1)]

    loads[0].wait()
    qz[z] = jnp.concatenate([q[0].astype(F32), q[1].astype(F32)], axis=1).astype(BF16)
    loads[1].wait()
    loads[2].wait()
    project(wo, g1, 1, gsend)
    loads[3].wait()
    loads[4].wait()
    project(wi, x1, 1, xsend)
    loads[5].wait()
    loads[6].wait()
    project(we, g0, 0, gsend)

    pl.semaphore_wait(barrier, len(peers))

    for n, o in enumerate(z_offsets):
        go(remote(qz.at[z], qz.at[z], qz_send.at[n], qz_recv.at[n], along_z(o)))
    g_in, x_in, t_in = [], [], []
    for r in range(1, MS):
        there = (m + r) % MS
        g_in.append(remote(gsend.at[there], grecv.at[r - 1], g_send.at[r - 1], g_recv.at[r - 1], in_plane(r)))
        x_in.append(remote(xsend.at[there], xrecv.at[r - 1], x_send.at[r - 1], x_recv.at[r - 1], in_plane(r)))
        t_in.append(remote(tsend.at[there], trecv.at[r - 1], x_send.at[r - 1], x_recv.at[r - 1], in_plane(r)))

    def layer_of(r):
        return ((m + r) % 4) // 2

    for r in range(1, MS):
        go(g_in[r - 1])

        @pl.when(layer_of(r) == 1)
        def _(r=r):
            x_in[r - 1].start()

    loads[7].wait()
    loads[8].wait()
    full = vt.shape[1] // BLK
    rest = vt.shape[1] - full * BLK
    last[...] = jnp.zeros(last.shape, BF16)
    last[:, :rest] = vt[:, full * BLK:]
    for b in range(full):
        table[b * 32:(b + 1) * 32, :] = vt[:, b * BLK:(b + 1) * BLK]
    table[full * 32:(full + 1) * 32, :] = last[...]
    local = ids[...] - m * vt.shape[1]
    for p in range(4):
        mine = local[:, 256 * p:256 * (p + 1)]
        low = mine & (BLK - 1)
        high = mine >> 9
        spot = lax.broadcasted_iota(jnp.int32, (BLK, 256), 0)
        hot = jnp.where(spot == low, 1.0, 0.0).astype(BF16)
        looked = dot_n(table[...], hot)
        total = jnp.zeros((32, 256), F32)
        for b in range(full + 1):
            total = total + jnp.where(high == b, looked[b * 32:(b + 1) * 32, :], 0.0)
        for h in range(2):
            seq = 2 * p + h
            tsend[(seq // 2) * 4 + seq % 2] = total[:, 128 * h:128 * (h + 1)].astype(BF16)
    for r in range(1, MS):
        @pl.when(layer_of(r) == 0)
        def _(r=r):
            t_in[r - 1].start()

    loads[9].wait()
    for n, o in enumerate(z_offsets):
        spot = qz.at[(z - o + ZS) % ZS]
        remote(spot, spot, qz_send.at[n], qz_recv.at[n], along_z(o)).wait_recv()
    legs = [(j, -REACH) for j in range(1, REACH + 1)] + [(-j, REACH) for j in range(1, REACH)]
    for n, (j, to) in enumerate(legs):
        spot = qz.at[(z + j + ZS) % ZS]
        go(remote(spot, spot, qz_send.at[8 + n], qz_recv.at[8 + n], along_z(to)))

    for copy in g_in:
        copy.wait_recv()

    @pl.when(layer == 1)
    def _():
        for copy in x_in:
            copy.wait_recv()
        total = xsend[m]
        for r in range(MS - 1):
            total = total + xrecv[r]
        xsum[...] = total

    @pl.when(layer == 0)
    def _():
        for copy in t_in:
            copy.wait_recv()
        total = tsend[m].astype(F32)
        for r in range(MS - 1):
            total = total + trecv[r].astype(F32)
        xsum[...] = total

    gsum = gsend[m]
    for r in range(MS - 1):
        gsum = gsum + grecv[r]
    lane8 = lax.broadcasted_iota(jnp.int32, (1, 8), 1)
    length = jnp.sum(jnp.where(lane8 == row, lens[...], 0), axis=1, keepdims=True)
    place = lax.broadcasted_iota(jnp.int32, (1, 128), 1)
    weight = jnp.where(place < length, 1.0 / length.astype(F32), 0.0)
    sk[...] = lax.dot_general(
        gsum * weight, xsum[...], (((1,), (1,)), ((), ())),
        precision=lax.Precision.HIGHEST, preferred_element_type=F32,
    )
    sz[4] = jnp.concatenate([sk[pl.ds(a, 8, stride=4), :] for a in range(4)], axis=1)

    def z_copy(t):
        slot = (4 - t) % ZS
        return remote(sz.at[4], sz.at[slot], sz_send.at[slot], sz_recv.at[slot], along_z(t))

    for t in [8] + [o for k in range(7, 0, -1) for o in (k, -k)]:
        go(z_copy(t))

    for n, (j, to) in enumerate(legs):
        spot = qz.at[(z - to + j + ZS) % ZS]
        remote(spot, spot, qz_send.at[8 + n], qz_recv.at[8 + n], along_z(to)).wait_recv()
    left = lax.broadcasted_iota(jnp.int32, (64, 128), 1) < 64
    first, second = qz[0:8].reshape(64, 128).astype(F32), qz[8:16].reshape(64, 128).astype(F32)
    qp[0] = jnp.where(left, first, pltpu.roll(second, 64, 1)).astype(BF16)
    qp[1] = jnp.where(left, pltpu.roll(first, 64, 1), second).astype(BF16)
    for r in range(1, MS):
        go(remote(qp.at[layer_of(r)], qg.at[m, core], qp_send.at[r - 1], qp_recv.at[r - 1], in_plane(r)))
    go(remote(qp.at[layer], qg.at[m, core], qs_send.at[0], qs_recv.at[0], sibling))
    qg[m, core] = qp[layer]

    def block_at(i, c, k):
        return shl.at[:, :, (2 * i + c) * 2 + k]

    def spread(k):
        for j in range(8 * k, 8 * k + 8):
            if j != 4:
                z_copy((4 - j) % ZS).wait_recv()
        for s in range(8):
            high, low = halves(sz[8 * k:8 * k + 8, s, :])
            shl[0, s, (2 * row + core) * 2 + k] = high
            shl[1, s, (2 * row + core) * 2 + k] = low
        block = block_at(row, core, k)
        for r in range(1, 8):
            go(remote(block, block, sp_send.at[k, r - 1], sp_recv.at[k, r - 1], in_group(r)))
        go(remote(block, block, ss_send.at[k, 0], ss_recv.at[k, 0], sibling))

    spread(0)

    for r in range(1, MS):
        block = qg.at[(m - r + MS) % MS, core]
        remote(qp.at[0], block, qp_send.at[r - 1], qp_recv.at[r - 1], in_plane(r)).wait_recv()
        go(remote(block, block, qs_send.at[r], qs_recv.at[r], sibling))

    spread(1)

    for r in range(MS):
        block = qg.at[(m - r + MS) % MS, 1 - core]
        remote(block, block, qs_send.at[r], qs_recv.at[r], sibling).wait_recv()
    for s in range(8):
        even, odd = [], []
        for c in range(2):
            a = qg[2 * s, c].astype(F32)
            b = qg[2 * s + 1, c].astype(F32)
            even.append(jnp.where(left, a, pltpu.roll(b, 64, 1)))
            odd.append(jnp.where(left, pltpu.roll(a, 64, 1), b))
        for h, both in enumerate((even, odd)):
            rows = [both[c][8 * k:8 * k + 8] for k in range(8) for c in range(2)]
            bt[128 * h:128 * h + 128, 128 * s:128 * (s + 1)] = jnp.concatenate(rows, axis=0).astype(BF16)

    square = bt[...].astype(F32)
    square_high, square_low = halves(square * square)
    ones = jnp.ones((8, 1024), BF16)
    bb[...] = dot_t(ones, square_high) + dot_t(ones, square_low)

    for k in range(2):
        for r in range(1, 8):
            block = block_at((row - r + 8) % 8, core, k)
            remote(block, block, sp_send.at[k, r - 1], sp_recv.at[k, r - 1], in_group(r)).wait_recv()
            go(remote(block, block, ss_send.at[k, r], ss_recv.at[k, r], sibling))
    for k in range(2):
        for r in range(8):
            block = block_at((row - r + 8) % 8, 1 - core, k)
            remote(block, block, ss_send.at[k, r], ss_recv.at[k, r], sibling).wait_recv()

    s_high = jnp.concatenate([shl[0, s].reshape(256, 128) for s in range(8)], axis=1)
    s_low = jnp.concatenate([shl[1, s].reshape(256, 128) for s in range(8)], axis=1)
    u = dot_t(s_high, bt[...]) + dot_t(s_low, bt[...])
    k_mat = dot_t(s_high, s_high) + dot_t(s_high, s_low) + dot_t(s_low, s_high)
    k_high, k_low = halves(k_mat)
    u_high, u_low = halves(u)
    v = dot_n(k_high, u_high) + dot_n(k_high, u_low) + dot_n(k_low, u_high)

    rr = bb[0:1, :]
    scaled = u * 0.0625
    uu = jnp.sum(scaled * scaled, axis=0, keepdims=True)
    step0 = rr / (uu + DAMPING * rr + EPSILON)
    keep = 1.0 - DAMPING * step0
    au = (step0 * 0.00390625) * u
    av = (step0 * 0.00390625) * v
    auu = step0 * uu
    aauv = jnp.sum(au * av, axis=0, keepdims=True)
    new = jnp.maximum(keep * keep * rr - 2.0 * keep * auu + aauv, 0.0)
    fac = keep + new / (rr + EPSILON)
    dd = jnp.maximum(fac * fac * rr - 2.0 * fac * auu + aauv, 0.0)
    y = fac * u - av
    scaled_y = y * 0.0625
    yy = jnp.sum(scaled_y * scaled_y, axis=0, keepdims=True)
    step1 = new / (yy + DAMPING * dd + EPSILON)
    scores = step0 * u + step1 * y
    rows = [
        jnp.concatenate([scores[32 * i + 16 * c + 4:32 * i + 16 * c + 5, :] for i in range(8)], axis=0)
        for c in range(2)
    ]
    part[...] = jnp.where(core == 0, rows[0], rows[1])

    final = remote(part, other, c_send.at[0], c_recv.at[0], partner)
    go(final)
    final.wait_recv()
    out_ref[...] = part[...] + other[...]
    for r in range(1, MS):
        @pl.when(layer_of(r) == 1)
        def _(r=r):
            x_in[r - 1].wait_send()

        @pl.when(layer_of(r) == 0)
        def _(r=r):
            t_in[r - 1].wait_send()
    for copy in sent:
        copy.wait_send()


def per_device(
    token_ids, lengths, embed_grads, vocab_basis, embed_basis,
    layer_inputs, layer_grads, input_basis, output_basis, queries,
):
    vocab = vocab_basis.shape[0]
    dma = pltpu.SemaphoreType.DMA
    return pl.pallas_call(
        kernel,
        out_shape=jax.ShapeDtypeStruct((8, 256), F32),
        in_specs=[pl.BlockSpec(memory_space=pl.ANY)] * 10,
        out_specs=pl.BlockSpec(memory_space=pltpu.VMEM),
        scratch_shapes=[
            pltpu.VMEM((1, 1024), jnp.int32),
            pltpu.VMEM((1, 8), jnp.int32),
            pltpu.VMEM((1024, 256), BF16),
            pltpu.VMEM((32, vocab), BF16),
            pltpu.VMEM((32, 256), BF16),
            pltpu.VMEM((1024, 256), BF16),
            pltpu.VMEM((1024, 256), BF16),
            pltpu.VMEM((32, 256), BF16),
            pltpu.VMEM((32, 256), BF16),
            pltpu.VMEM((2, 8, 64), BF16),
            pltpu.VMEM((32, BLK), BF16),
            pltpu.VMEM((512, BLK), BF16),
            pltpu.VMEM((MS, 32, 128), F32),
            pltpu.VMEM((MS, 32, 128), F32),
            pltpu.VMEM((MS, 32, 128), BF16),
            pltpu.VMEM((MS - 1, 32, 128), F32),
            pltpu.VMEM((MS - 1, 32, 128), F32),
            pltpu.VMEM((MS - 1, 32, 128), BF16),
            pltpu.VMEM((32, 128), F32),
            pltpu.VMEM((32, 32), F32),
            pltpu.VMEM((ZS, 8, 128), BF16),
            pltpu.VMEM((2, 64, 128), BF16),
            pltpu.VMEM((MS, 2, 64, 128), BF16),
            pltpu.VMEM((ZS, 8, 128), F32),
            pltpu.VMEM((2, 8, 32, 8, 128), BF16),
            pltpu.VMEM((256, 1024), BF16),
            pltpu.VMEM((8, 256), F32),
            pltpu.VMEM((8, 256), F32),
            pltpu.VMEM((8, 256), F32),
            dma((10,)),
            dma((MS - 1,)), dma((MS - 1,)), dma((MS - 1,)), dma((MS - 1,)),
            dma((15,)), dma((15,)),
            dma((MS - 1,)), dma((MS - 1,)),
            dma((MS,)), dma((MS,)),
            dma((ZS,)), dma((ZS,)),
            dma((2, 7)), dma((2, 7)),
            dma((2, 8)), dma((2, 8)),
            dma((1,)), dma((1,)),
        ],
        compiler_params=pltpu.CompilerParams(
            collective_id=0, has_side_effects=True
        ),
        name="attribution",
    )(
        token_ids.reshape(1, -1), lengths.reshape(1, -1), embed_grads, vocab_basis.T, embed_basis.T,
        layer_inputs[0], layer_grads[0], input_basis[0].T, output_basis[0].T,
        queries.transpose(0, 2, 1),
    )


def solution(mesh):
    placed = (
        P("dp"),
        P("dp"),
        P("dp", "mp"),
        P("mp", None),
        P("mp", None),
        P(None, "dp", "mp"),
        P(None, "dp", "mp"),
        P(None, "mp", None),
        P(None, "mp", None),
        P(None, "mp", "dp"),
    )
    return jax.shard_map(
        per_device, mesh=mesh, in_specs=placed, out_specs=P("dp", None), check_vma=False
    )
```

time: 58 us -> 46.6 us (0.80)
  local copies, waits for them, and re-layouts: 8.29 us -> 1.3 us
  Pallas kernels: 49.2 us -> 45 us
    unnamed x21 -> x1, local copies, waits for them, and re-layouts: 8.29 us -> 1.3 us
    pallas_call x1, Pallas kernels: 49.2 us -> 45 us  [per_device(): pl.pallas_call(kernel, out_shape=jax.ShapeDtypeStruct((8, 256), F32), in_...]
where the time goes in v2:
time: 46.6 us; the launch traced here: 46.3 us
  Pallas kernels  45 us (97%)
  local copies, waits for them, and re-layouts  1.3 us (3%)
    pallas_call x1, Pallas kernels, per_device(): pl.pallas_call(kernel, out_shape=jax.ShapeDtypeStruct((8, 256), F32), in_...  45 us
    unnamed x1, local copies, waits for them, and re-layouts  1.3 us

profile of v2, /device:TPU:1, one launch (start us, length us, event | category | flops | bytes accessed | tf_op | source)
XLA Modules:
  0.0 46.3 jit_solution(12587765414624954537)
XLA Ops:
  0.0 45.0 %attribution.1 = f32[8,256]{1,0:T(8,128)} custom-call(s32[1,1024]{1,0:T(1,128)} %bitcast.19, s32[1,8]{1,0:T(1,128)} %bitcast.21, bf16[1024,256]{1,0:T(8,128)(2,1)} %g0_hbm.1, bf16[32,8016]{1,0:T(8,128)(2,1)} %bitcast.15, bf16[32,256]{1,0:T(8,128)(2,1)} %bitcast.16, bf16[1024,256]{1,0:T(8,128)(2,1)} %bitcast.13, bf16[1024,256]{1,0:T(8,128)(2,1)} %bitcast.14, ...), custom_call_target="tpu_custom_call" | custom-call | tf_op jit(solution)/shard_map/attribution/pallas_call | solution.py:324
  45.0 1.3 %copy.12 = f32[8,256]{1,0:T(8,128)} copy(f32[8,256]{1,0:T(8,128)} %attribution.1) | data formatting | bytes 16384

commit v3 on v2

--- a/solution.py
+++ b/solution.py
@@ -36,7 +36,7 @@
     ids, lens, g0, vt, we, x1, g1, wi, wo, q,
     last, table, gsend, xsend, tsend, grecv, xrecv, trecv, xsum, sk,
     qz, qp, qg, sz, shl, bt, bb, part, other,
-    in_sem, g_send, g_recv, x_send, x_recv, qz_send, qz_recv, qp_send, qp_recv, qs_send, qs_recv,
+    in_sem, g_send, g_recv, x_send, t_send, x_recv, qz_send, qz_recv, qp_send, qp_recv, qs_send, qs_recv,
     sz_send, sz_recv, sp_send, sp_recv, ss_send, ss_recv, c_send, c_recv,
 ):
     d = lax.axis_index("dp")
@@ -44,20 +44,34 @@
     core = d % 2
     z = d // 2
     x = m % 4
+    y = m // 4
     layer = x // 2
-    row = (m // 4) * 2 + x % 2
+    row = y * 2 + x % 2
     sibling = (d + 1 - 2 * core, m)
     partner = (d, m - x + 3 - x)
 
     def along_z(offset):
         return (2 * ((z + offset + ZS) % ZS) + core, m)
 
-    def in_plane(r):
-        return (d, (m + r) % MS)
-
-    def in_group(r):
-        there = (row + r) % 8
-        return (d, (there // 2) * 4 + 2 * layer + there % 2)
+    def hops(k):
+        return min(k, 4 - k)
+
+    plane = sorted(((i, j) for i in range(4) for j in range(4) if i or j), key=lambda k: -hops(k[0]) - hops(k[1]))
+
+    def there_of(i, j):
+        return (y + j) % 4 * 4 + (x + i) % 4
+
+    def layer_of(i):
+        return (x + i) % 4 // 2
+
+    group = sorted(((i, j) for i in range(2) for j in range(4) if i or j), key=lambda k: -k[0] - hops(k[1]))
+    odd_x = x % 2
+
+    def group_row(i, j):
+        return (y + j + 4) % 4 * 2 + (odd_x + i) % 2
+
+    def in_group(i, j):
+        return (d, (y + j) % 4 * 4 + 2 * layer + (odd_x + i) % 2)
 
     pairs = [
         (q_hbm, q), (wo_hbm, wo), (g1_hbm, g1), (wi_hbm, wi), (x1_hbm, x1),
@@ -70,7 +84,7 @@
 
     barrier = pltpu.get_barrier_semaphore()
     z_offsets = [o for k in range(REACH, 0, -1) for o in (k, -k)]
-    peers = [along_z(o) for o in z_offsets] + [in_plane(r) for r in range(1, MS)] + [sibling]
+    peers = [along_z(o) for o in z_offsets] + [(d, there_of(i, j)) for i, j in plane] + [sibling]
     for peer in peers:
         pl.semaphore_signal(barrier, inc=1, device_id=peer, device_id_type=MESH)
 
@@ -80,11 +94,11 @@
             device_id=peer, device_id_type=MESH,
         )
 
-    sent = []
-
-    def go(copy):
-        copy.start()
-        sent.append(copy)
+    def take(sem, whole):
+        remote(whole, whole, sem, sem, sibling).wait_recv()
+
+    def drain(sem, whole):
+        remote(whole, whole, sem, sem, sibling).wait_send()
 
     def project(basis, tokens, layer_at, target):
         out = dot_t(basis[...], tokens[...])
@@ -105,24 +119,15 @@
 
     pl.semaphore_wait(barrier, len(peers))
 
-    for n, o in enumerate(z_offsets):
-        go(remote(qz.at[z], qz.at[z], qz_send.at[n], qz_recv.at[n], along_z(o)))
-    g_in, x_in, t_in = [], [], []
-    for r in range(1, MS):
-        there = (m + r) % MS
-        g_in.append(remote(gsend.at[there], grecv.at[r - 1], g_send.at[r - 1], g_recv.at[r - 1], in_plane(r)))
-        x_in.append(remote(xsend.at[there], xrecv.at[r - 1], x_send.at[r - 1], x_recv.at[r - 1], in_plane(r)))
-        t_in.append(remote(tsend.at[there], trecv.at[r - 1], x_send.at[r - 1], x_recv.at[r - 1], in_plane(r)))
-
-    def layer_of(r):
-        return ((m + r) % 4) // 2
-
-    for r in range(1, MS):
-        go(g_in[r - 1])
-
-        @pl.when(layer_of(r) == 1)
-        def _(r=r):
-            x_in[r - 1].start()
+    for o in z_offsets:
+        remote(qz.at[z], qz.at[z], qz_send.at[0], qz_recv.at[0], along_z(o)).start()
+    for r, (i, j) in enumerate(plane):
+        there = there_of(i, j)
+        remote(gsend.at[there], grecv.at[r], g_send, g_recv, (d, there)).start()
+
+        @pl.when(layer_of(i) == 1)
+        def _(r=r, there=there):
+            remote(xsend.at[there], xrecv.at[r], x_send, x_recv, (d, there)).start()
 
     loads[7].wait()
     loads[8].wait()
@@ -147,27 +152,25 @@
         for h in range(2):
             seq = 2 * p + h
             tsend[(seq // 2) * 4 + seq % 2] = total[:, 128 * h:128 * (h + 1)].astype(BF16)
-    for r in range(1, MS):
-        @pl.when(layer_of(r) == 0)
-        def _(r=r):
-            t_in[r - 1].start()
+    for r, (i, j) in enumerate(plane):
+        there = there_of(i, j)
+
+        @pl.when(layer_of(i) == 0)
+        def _(r=r, there=there):
+            remote(tsend.at[there], trecv.at[r], t_send, x_recv, (d, there)).start()
 
     loads[9].wait()
-    for n, o in enumerate(z_offsets):
-        spot = qz.at[(z - o + ZS) % ZS]
-        remote(spot, spot, qz_send.at[n], qz_recv.at[n], along_z(o)).wait_recv()
-    legs = [(j, -REACH) for j in range(1, REACH + 1)] + [(-j, REACH) for j in range(1, REACH)]
-    for n, (j, to) in enumerate(legs):
-        spot = qz.at[(z + j + ZS) % ZS]
-        go(remote(spot, spot, qz_send.at[8 + n], qz_recv.at[8 + n], along_z(to)))
-
-    for copy in g_in:
-        copy.wait_recv()
+    take(qz_recv.at[0], qz.at[0:8])
+    legs = [(k, -REACH) for k in range(1, REACH + 1)] + [(-k, REACH) for k in range(1, REACH)]
+    for k, to in legs:
+        spot = qz.at[(z + k + ZS) % ZS]
+        remote(spot, spot, qz_send.at[1], qz_recv.at[1], along_z(to)).start()
+
+    take(g_recv, grecv)
 
     @pl.when(layer == 1)
     def _():
-        for copy in x_in:
-            copy.wait_recv()
+        take(x_recv, xrecv)
         total = xsend[m]
         for r in range(MS - 1):
             total = total + xrecv[r]
@@ -175,8 +178,7 @@
 
     @pl.when(layer == 0)
     def _():
-        for copy in t_in:
-            copy.wait_recv()
+        take(x_recv, trecv)
         total = tsend[m].astype(F32)
         for r in range(MS - 1):
             total = total + trecv[r].astype(F32)
@@ -195,53 +197,41 @@
     )
     sz[4] = jnp.concatenate([sk[pl.ds(a, 8, stride=4), :] for a in range(4)], axis=1)
 
-    def z_copy(t):
+    for t in [8] + [o for k in (1, 7, 2, 6, 3, 5, 4) for o in (k, -k)]:
         slot = (4 - t) % ZS
-        return remote(sz.at[4], sz.at[slot], sz_send.at[slot], sz_recv.at[slot], along_z(t))
-
-    for t in [8] + [o for k in range(7, 0, -1) for o in (k, -k)]:
-        go(z_copy(t))
-
-    for n, (j, to) in enumerate(legs):
-        spot = qz.at[(z - to + j + ZS) % ZS]
-        remote(spot, spot, qz_send.at[8 + n], qz_recv.at[8 + n], along_z(to)).wait_recv()
+        remote(sz.at[4], sz.at[slot], sz_send, sz_recv.at[slot // 8], along_z(t)).start()
+
+    take(qz_recv.at[1], qz.at[0:7])
     left = lax.broadcasted_iota(jnp.int32, (64, 128), 1) < 64
     first, second = qz[0:8].reshape(64, 128).astype(F32), qz[8:16].reshape(64, 128).astype(F32)
     qp[0] = jnp.where(left, first, pltpu.roll(second, 64, 1)).astype(BF16)
     qp[1] = jnp.where(left, pltpu.roll(first, 64, 1), second).astype(BF16)
-    for r in range(1, MS):
-        go(remote(qp.at[layer_of(r)], qg.at[m, core], qp_send.at[r - 1], qp_recv.at[r - 1], in_plane(r)))
-    go(remote(qp.at[layer], qg.at[m, core], qs_send.at[0], qs_recv.at[0], sibling))
+    for i, j in plane:
+        remote(qp.at[layer_of(i)], qg.at[m, core], qp_send, qp_recv, (d, there_of(i, j))).start()
     qg[m, core] = qp[layer]
 
     def block_at(i, c, k):
         return shl.at[:, :, (2 * i + c) * 2 + k]
 
     def spread(k):
-        for j in range(8 * k, 8 * k + 8):
-            if j != 4:
-                z_copy((4 - j) % ZS).wait_recv()
+        take(sz_recv.at[k], sz.at[0:7] if k == 0 else sz.at[0:8])
         for s in range(8):
             high, low = halves(sz[8 * k:8 * k + 8, s, :])
             shl[0, s, (2 * row + core) * 2 + k] = high
             shl[1, s, (2 * row + core) * 2 + k] = low
         block = block_at(row, core, k)
-        for r in range(1, 8):
-            go(remote(block, block, sp_send.at[k, r - 1], sp_recv.at[k, r - 1], in_group(r)))
-        go(remote(block, block, ss_send.at[k, 0], ss_recv.at[k, 0], sibling))
+        for r, (i, j) in enumerate(group):
+            remote(block, block, sp_send, sp_recv.at[k, r], in_group(i, j)).start()
+        remote(block, block, ss_send, ss_recv.at[k], sibling).start()
 
     spread(0)
 
-    for r in range(1, MS):
-        block = qg.at[(m - r + MS) % MS, core]
-        remote(qp.at[0], block, qp_send.at[r - 1], qp_recv.at[r - 1], in_plane(r)).wait_recv()
-        go(remote(block, block, qs_send.at[r], qs_recv.at[r], sibling))
+    take(qp_recv, qg.at[0:15, core])
+    remote(qg.at[:, core], qg.at[:, core], qs_send, qs_recv, sibling).start()
 
     spread(1)
 
-    for r in range(MS):
-        block = qg.at[(m - r + MS) % MS, 1 - core]
-        remote(block, block, qs_send.at[r], qs_recv.at[r], sibling).wait_recv()
+    take(qs_recv, qg.at[:, 1 - core])
     for s in range(8):
         even, odd = [], []
         for c in range(2):
@@ -259,14 +249,12 @@
     bb[...] = dot_t(ones, square_high) + dot_t(ones, square_low)
 
     for k in range(2):
-        for r in range(1, 8):
-            block = block_at((row - r + 8) % 8, core, k)
-            remote(block, block, sp_send.at[k, r - 1], sp_recv.at[k, r - 1], in_group(r)).wait_recv()
-            go(remote(block, block, ss_send.at[k, r], ss_recv.at[k, r], sibling))
+        for r, (i, j) in enumerate(group):
+            block = block_at(group_row(i, -j), core, k)
+            take(sp_recv.at[k, r], block)
+            remote(block, block, ss_send, ss_recv.at[k], sibling).start()
     for k in range(2):
-        for r in range(8):
-            block = block_at((row - r + 8) % 8, 1 - core, k)
-            remote(block, block, ss_send.at[k, r], ss_recv.at[k, r], sibling).wait_recv()
+        take(ss_recv.at[k], shl.at[:, :, 0:8])
 
     s_high = jnp.concatenate([shl[0, s].reshape(256, 128) for s in range(8)], axis=1)
     s_low = jnp.concatenate([shl[1, s].reshape(256, 128) for s in range(8)], axis=1)
@@ -299,20 +287,29 @@
     ]
     part[...] = jnp.where(core == 0, rows[0], rows[1])
 
-    final = remote(part, other, c_send.at[0], c_recv.at[0], partner)
-    go(final)
+    final = remote(part, other, c_send, c_recv, partner)
+    final.start()
     final.wait_recv()
     out_ref[...] = part[...] + other[...]
-    for r in range(1, MS):
-        @pl.when(layer_of(r) == 1)
-        def _(r=r):
-            x_in[r - 1].wait_send()
-
-        @pl.when(layer_of(r) == 0)
-        def _(r=r):
-            t_in[r - 1].wait_send()
-    for copy in sent:
-        copy.wait_send()
+    final.wait_send()
+    drain(qz_send.at[0], qz.at[0:8])
+    drain(qz_send.at[1], qz.at[0:7])
+    drain(g_send, grecv)
+    drain(sz_send, sz.at[0:15])
+    drain(qp_send, qg.at[0:15, core])
+    drain(qs_send, qg.at[:, core])
+    drain(sp_send, shl.at[:, :, 0:14])
+    drain(ss_send, shl.at[:, :, 0:16])
+
+    @pl.when(layer == 1)
+    def _():
+        drain(x_send, xsend.at[0:7])
+        drain(t_send, tsend.at[0:8])
+
+    @pl.when(layer == 0)
+    def _():
+        drain(x_send, xsend.at[0:8])
+        drain(t_send, tsend.at[0:7])
 
 
 def per_device(
@@ -323,7 +320,7 @@
     dma = pltpu.SemaphoreType.DMA
     return pl.pallas_call(
         kernel,
-        out_shape=jax.ShapeDtypeStruct((8, 256), F32),
+        out_shape=pltpu.VMEM((8, 256), F32),
         in_specs=[pl.BlockSpec(memory_space=pl.ANY)] * 10,
         out_specs=pl.BlockSpec(memory_space=pltpu.VMEM),
         scratch_shapes=[
@@ -357,14 +354,13 @@
             pltpu.VMEM((8, 256), F32),
             pltpu.VMEM((8, 256), F32),
             dma((10,)),
-            dma((MS - 1,)), dma((MS - 1,)), dma((MS - 1,)), dma((MS - 1,)),
-            dma((15,)), dma((15,)),
-            dma((MS - 1,)), dma((MS - 1,)),
-            dma((MS,)), dma((MS,)),
-            dma((ZS,)), dma((ZS,)),
-            dma((2, 7)), dma((2, 7)),
-            dma((2, 8)), dma((2, 8)),
-            dma((1,)), dma((1,)),
+            dma, dma, dma, dma, dma,
+            dma((2,)), dma((2,)),
+            dma, dma, dma, dma,
+            dma, dma((2,)),
+            dma, dma((2, 7)),
+            dma, dma((2,)),
+            dma, dma,
         ],
         compiler_params=pltpu.CompilerParams(
             collective_id=0, has_side_effects=True

time: 46.6 us -> 42.1 us (0.903)
  Pallas kernels: 45 us -> 41.4 us
  local copies, waits for them, and re-layouts: 1.3 us -> 0.6 us
    pallas_call x1, Pallas kernels: 45 us -> 41.4 us  [per_device(): pl.pallas_call(kernel, out_shape=pltpu.VMEM((8, 256), F32), in_specs=[pl....]
    unnamed x1, local copies, waits for them, and re-layouts: 1.3 us -> 0.6 us
where the time goes in v3:
time: 42.1 us; the launch traced here: 42 us
  Pallas kernels  41.4 us (98%)
  local copies, waits for them, and re-layouts  0.6 us (1%)
    pallas_call x1, Pallas kernels, per_device(): pl.pallas_call(kernel, out_shape=pltpu.VMEM((8, 256), F32), in_specs=[pl....  41.4 us

profile of v3, /device:TPU:1, one launch (start us, length us, event | category | flops | bytes accessed | tf_op | source)
XLA Modules:
  0.0 42.0 jit_solution(13264124087775177341)
XLA Ops:
  0.0 41.4 %attribution.1 = f32[8,256]{1,0:T(8,128)S(1)} custom-call(s32[1,1024]{1,0:T(1,128)} %bitcast.19, s32[1,8]{1,0:T(1,128)} %bitcast.21, bf16[1024,256]{1,0:T(8,128)(2,1)} %g0_hbm.1, bf16[32,8016]{1,0:T(8,128)(2,1)} %bitcast.15, bf16[32,256]{1,0:T(8,128)(2,1)} %bitcast.16, bf16[1024,256]{1,0:T(8,128)(2,1)} %bitcast.13, bf16[1024,256]{1,0:T(8,128)(2,1)} %bitcast.14, ...), custom_call_target="tpu_custom_call" | custom-call | tf_op jit(solution)/shard_map/attribution/pallas_call | solution.py:321
  41.4 0.6 %copy.12 = f32[8,256]{1,0:T(8,128)} copy(f32[8,256]{1,0:T(8,128)S(1)} %attribution.1) | data formatting | bytes 16384
